TPU v7x, 32 devices: a whole 2x2x4 slice. The times are simulated.
32 devices in a mesh: dp: 4 (over y, core), seq: 8 (over z, x).
Axes of the slice: x: 2, y: 2, z: 4, core: 2. Of those that a mesh axis runs over, the one named last changes fastest.
Arguments:
- queries: bfloat16 [4, 1024, 2048], P('dp', 'seq'), may hold values from -12 to 12
- keys: bfloat16 [4, 1024, 512], P('dp', 'seq'), may hold values from -4 to 4
- values: bfloat16 [4, 1024, 512], P('dp', 'seq'), may hold values from -6 to 6
- segments: int32 [4, 1024], P('dp', 'seq'), may hold values from 0 to 3, never falling along the last dimension, each value on 1 to 896 neighbouring positions
- task_ids: int32 [4], replicated, may hold values from 0 to 15
- prompt_keys: bfloat16 [16, 128, 512], P('seq'), may hold values from -4 to 4
- prompt_values: bfloat16 [16, 128, 512], P('seq'), may hold values from -6 to 6
- grad_out: bfloat16 [4, 1024, 2048], P('dp', 'seq'), may hold values from -6 to 6
Outputs:
- attended: bfloat16 [4, 1024, 2048], P('dp', 'seq')
- prompt_key_grad: float32 [16, 128, 512], P('seq')
- prompt_value_grad: float32 [16, 128, 512], P('seq')
Inputs may be any that keep to these rules, and one draw needn't show every extreme that they name: `segments`: along each example the document numbers never fall; one document holds 896 tokens.
All inputs are finite; a program needn't handle non-finite values.
Results may differ from a plain program's by a relative error of at most 0.0096.
Values may be sent and summed in bfloat16 or wider, within the bound.
A program may use at most 128 MiB of HBM per device.

v0:
```python
import math

import jax
import jax.numpy as jnp
from jax import lax
from jax.sharding import PartitionSpec as P

KVH = 4
GROUP = 4
HD = 128
PROMPT = 128


def spread(value, axis, source):
    kept = jnp.where(lax.axis_index(axis) == source, value, 0).astype(value.dtype)
    return lax.psum(kept, axis)


def shards(queries, keys, values, segments, task_ids, prompt_keys, prompt_values, grad_out):
    tok_rows = queries.shape[1]
    scaling = 1.0 / math.sqrt(HD)
    seq_rank = lax.axis_index("seq")
    query_heads = queries[0].reshape(tok_rows, KVH, GROUP, HD)
    query_segments = segments[0]
    query_index = seq_rank * tok_rows + lax.iota(jnp.int32, tok_rows)
    all_segments = lax.all_gather(segments[0], "seq", axis=0, tiled=True)
    bank_size = prompt_keys.shape[0]
    my_task = task_ids[lax.axis_index("dp")]
    prompt_owner = my_task // bank_size
    bank_slot = my_task % bank_size
    local_pair = jnp.stack(
        [
            lax.dynamic_index_in_dim(prompt_keys, bank_slot, 0, keepdims=False),
            lax.dynamic_index_in_dim(prompt_values, bank_slot, 0, keepdims=False),
        ]
    )
    shared_pair = spread(local_pair, "seq", prompt_owner)
    prompt_key_heads = shared_pair[0].reshape(PROMPT, KVH, HD)
    prompt_value_heads = shared_pair[1].reshape(PROMPT, KVH, HD)
    prompt_scores = (
        jnp.einsum(
            "tkgd,pkd->tkgp", query_heads, prompt_key_heads, preferred_element_type=jnp.float32
        )
        * scaling
    )
    maximum = jnp.max(prompt_scores, axis=-1)
    weights = jnp.exp(prompt_scores - maximum[..., None])
    totals = jnp.sum(weights, axis=-1)
    accumulated = jnp.einsum(
        "tkgp,pkd->tkgd",
        weights.astype(jnp.bfloat16),
        prompt_value_heads,
        preferred_element_type=jnp.float32,
    )
    carried = (maximum, totals, accumulated)

    def absorb_rows(state_now, stacked, first_row):
        key_count = stacked.shape[1]
        key_index = first_row + lax.iota(jnp.int32, key_count)
        key_segments = lax.dynamic_slice_in_dim(
            all_segments, jnp.maximum(first_row, 0), key_count, 0
        )
        key_mask = (
            (key_segments[None, :] == query_segments[:, None])
            & (key_index[None, :] <= query_index[:, None])
            & True
        )

        def update(inner_state):
            old_peak, old_totals, old_accum = inner_state
            key_heads = stacked[0].reshape(key_count, KVH, HD)
            value_heads = stacked[1].reshape(key_count, KVH, HD)
            scores = (
                jnp.einsum(
                    "tkgd,skd->tkgs", query_heads, key_heads, preferred_element_type=jnp.float32
                )
                * scaling
            )
            mask_wide = key_mask[:, None, None, :]
            new_peak = jnp.maximum(
                old_peak, jnp.max(jnp.where(mask_wide, scores, -jnp.inf), axis=-1)
            )
            shrink = jnp.exp(old_peak - new_peak)
            block_weights = jnp.where(mask_wide, jnp.exp(scores - new_peak[..., None]), 0.0)
            new_totals = old_totals * shrink + jnp.sum(block_weights, axis=-1)
            new_accum = old_accum * shrink[..., None] + jnp.einsum(
                "tkgs,skd->tkgd",
                block_weights.astype(jnp.bfloat16),
                value_heads,
                preferred_element_type=jnp.float32,
            )
            return (new_peak, new_totals, new_accum)

        return lax.cond(jnp.any(key_mask), update, lambda inner_state: inner_state, state_now)

    own_pair = jnp.stack([keys[0], values[0]])
    stacked = lax.all_gather(own_pair, "seq", axis=1, tiled=True)
    key_count = stacked.shape[1]
    tile_rows = 512

    def loop_tile(block_index, inner_state):
        offset = block_index * tile_rows
        piece = lax.dynamic_slice_in_dim(stacked, offset, tile_rows, 1)
        return absorb_rows(inner_state, piece, offset)

    carried = lax.fori_loop(0, key_count // tile_rows, loop_tile, carried)
    maximum, totals, accumulated = carried
    attended = (accumulated / totals[..., None]).astype(jnp.bfloat16)
    log_norm = maximum + jnp.log(totals)
    grad_heads = grad_out[0].reshape(tok_rows, KVH, GROUP, HD)
    attended_wide = lax.optimization_barrier(attended).astype(jnp.float32)
    row_delta = jnp.sum(grad_heads.astype(jnp.float32) * attended_wide, axis=-1)
    prompt_probs = jnp.exp(prompt_scores - log_norm[..., None])
    prompt_dots = jnp.einsum(
        "tkgd,pkd->tkgp", grad_heads, prompt_value_heads, preferred_element_type=jnp.float32
    )
    score_grad = prompt_probs * (prompt_dots - row_delta[..., None])
    value_part = jnp.einsum(
        "tkgp,tkgd->pkd",
        prompt_probs.astype(jnp.bfloat16),
        grad_heads,
        preferred_element_type=jnp.float32,
    )
    key_part = (
        jnp.einsum(
            "tkgp,tkgd->pkd",
            score_grad.astype(jnp.bfloat16),
            query_heads,
            preferred_element_type=jnp.float32,
        )
        * scaling
    )
    value_part = value_part.reshape(PROMPT, KVH * HD)
    key_part = key_part.reshape(PROMPT, KVH * HD)
    key_sum, value_sum = lax.psum((key_part, value_part), "seq")
    key_all, value_all = (
        lax.all_gather(key_sum[None].astype(jnp.bfloat16), "dp", axis=0, tiled=True).astype(
            jnp.float32
        ),
        lax.all_gather(value_sum[None].astype(jnp.bfloat16), "dp", axis=0, tiled=True).astype(
            jnp.float32
        ),
    )
    own_tasks = seq_rank * bank_size + lax.iota(jnp.int32, bank_size)
    matches = (task_ids[:, None] == own_tasks[None, :])[:, :, None, None]
    key_grad = jnp.sum(jnp.where(matches, key_all[:, None], 0.0), axis=0)
    value_grad = jnp.sum(jnp.where(matches, value_all[:, None], 0.0), axis=0)
    return (attended.reshape(1, tok_rows, KVH * GROUP * HD), key_grad, value_grad)


def solution(mesh):
    in_specs = (
        P("dp", "seq", None),
        P("dp", "seq", None),
        P("dp", "seq", None),
        P("dp", "seq"),
        P(),
        P("seq", None, None),
        P("seq", None, None),
        P("dp", "seq", None),
    )
    out_specs = (P("dp", "seq", None), P("seq", None, None), P("seq", None, None))
    return jax.shard_map(shards, mesh=mesh, in_specs=in_specs, out_specs=out_specs, check_vma=False)
```

profile of v0, /device:TPU:1, one launch (start us, length us, event | category | flops | bytes accessed | tf_op | source)
XLA Modules:
  0.0 222.6 jit_solution(11185119642300208240)
XLA Ops:
  7.2 1.3 dynamic_slice.28
  11.1 1.0 constant_dynamic-slice_fusion.2
  12.4 0.7 maximum_select_fusion
  13.2 1.0 copy.52
  14.3 1.0 copy.51
  15.3 0.7 pad_maximum_fusion
  16.0 1.3 copy.47
  17.9 17.9 %all-gather = s32[1,1024]{1,0:T(1,128)S(1)} all-gather(s32[1,128]{1,0:T(1,128)S(1)} %copy-done.3), channel_id=2, replica_groups=mesh['dp'=4,'seq'=8] {'seq'}, dimensions={1}, use_global_device_ids=true | all-gather | bytes 4608 | tf_op jit(solution)/shard_map/all_gather | solution.py:26
  35.9 48.7 %all-reduce.4.cloned.1.call-done = bf16[2,128,512]{1,2,0:T(8,128)(2,1)} async-done(((bf16[2,128,512]{1,2,0:T(8,128)(2,1)}), bf16[2,128,512]{1,2,0:T(8,128)(2,1)}) %all-reduce.4.cloned.1.call-update) | async-done | bytes 262160 | tf_op jit(solution)/shard_map/psum | solution.py:16
  84.6 1.0 fusion.39
  85.6 0.4 fusion.40
  85.9 1.3 convolution_bitcast_fusion.1
  87.2 2.5 %copy.53 = f32[128,4,4,128]{3,0,2,1:T(8,128)} copy(f32[128,4,4,128]{0,3,2,1:T(8,128)} %convolution_bitcast_fusion.1) | data formatting | bytes 2097152
  90.0 47.8 %all-gather.5.cloned.1.call-done = bf16[2,1024,512]{1,2,0:T(8,128)(2,1)} async-done(((bf16[2,128,512]{1,2,0:T(8,128)(2,1)}), bf16[2,1024,512]{1,2,0:T(8,128)(2,1)}) %all-gather.5.cloned.1.call-update) | async-done | bytes 2097168 | tf_op jit(solution)/shard_map/all_gather | solution.py:97
  137.8 8.8 %while.18 = (s32[]{:T(128)}, f32[128,4,4]{0,2,1:T(4,128)S(1)}, f32[128,4,4]{0,2,1:T(4,128)S(1)}, f32[128,4,4,128]{3,0,2,1:T(8,128)}, s32[1024]{0:T(1024)S(1)}, /...) while((s32[]{:T(128)}, f32[128,4,4]{0,2,1:T(4,128)S(1)}, ...), condition=%wide.region_9.10_spmd.clone, body=%wide.region_3.9_spmd.clone.sunk | while | flops 549196416 | bytes 27144068 | solution.py:106
  137.8 0.8 fusion.52
  139.3 5.6 %conditional.3 = ((f32[128,4,4]{0,2,1:T(4,128)S(1)}, f32[128,4,4]{0,2,1:T(4,128)S(1)}, f32[128,4,4,128]{3,0,2,1:T(8,128)})) conditional(s32[]{:T(128)} %convert_element_type.85, (f32[128,4,4]{0,2,1:T(4,128)S(1)}, f32[128,4,4]{0,2,1:T(4,128)S(1)}, f32[128,4,4,128]{3,0,2,1:T(8,128)}) %tuple.65, (pred[128,512]{0,1:T(8,128)(4,1)S(1)}, s32[]{:T(128)}, ...), branch_computations={%region_5.5_spmd, %region_6.8_spmd} | conditional | flops 548933632 | bytes 27066510 | solution.py:94
  139.4 1.3 constant_dynamic-slice_fusion.1
  140.7 0.9 fusion.2
  141.5 0.9 fusion.6
  142.4 1.5 fusion.16
  144.0 1.0 copy-done.1
  145.0 0.8 fusion.52
  146.5 2.6 %copy.55 = f32[128,4,4,128]{0,3,2,1:T(8,128)} copy(f32[128,4,4,128]{3,0,2,1:T(8,128)} %get-tuple-element.225) | data formatting | bytes 2097152 | tf_op jit(solution)/shard_map/while | solution.py:106
  149.1 1.3 divide_convert_fusion
  150.4 1.0 copy.63
  151.6 0.3 fusion.31
  151.9 0.6 fusion.27
  152.5 40.1 %all-reduce.5 = (bf16[128,512]{0,1:T(8,128)(2,1)S(1)}, bf16[128,512]{0,1:T(8,128)(2,1)S(1)}) all-reduce(f32[128,512]{0,1:T(8,128)S(1)} %bitcast.123, f32[128,512]{0,1:T(8,128)S(1)} %bitcast.122), channel_id=1, replica_groups=mesh['dp'=4,'seq'=8] {'seq'}, use_global_device_ids=true, to_apply=%region_11.12 | all-reduce | flops 131072 | bytes 786432 | tf_op jit(solution)/shard_map/psum | solution.py:135
  192.6 14.2 %all-gather.2 = bf16[512,512]{0,1:T(8,128)(2,1)S(1)} all-gather(bf16[128,512]{0,1:T(8,128)(2,1)S(1)} %get-tuple-element.306), channel_id=4, replica_groups=mesh['dp'=4,'seq'=8] {'dp'}, dimensions={0}, use_global_device_ids=true | all-gather | bytes 655360 | tf_op jit(solution)/shard_map/all_gather | solution.py:140
  207.0 7.3 %all-gather.1 = bf16[512,512]{0,1:T(8,128)(2,1)S(1)} all-gather(bf16[128,512]{0,1:T(8,128)(2,1)S(1)} %get-tuple-element.305), channel_id=3, replica_groups=mesh['dp'=4,'seq'=8] {'dp'}, dimensions={0}, use_global_device_ids=true | all-gather | bytes 655360 | tf_op jit(solution)/shard_map/all_gather | solution.py:137
  214.5 1.3 select_reduce_fusion
  (34 shorter events, 2.0 us)
Async XLA Ops:
  7.2 28.6 %copy-start.4 = (s32[4]{0:T(128)S(1)}, s32[4]{0:T(128)}, u32[]{:S(2)}) copy-start(s32[4]{0:T(128)} %param.16) | copy-start | bytes 52
  7.2 10.5 %copy-start.2 = (bf16[1,128,2048]{2,1,0:T(8,128)(2,1)S(1)}, bf16[1,128,2048]{2,1,0:T(8,128)(2,1)}, u32[]{:S(2)}) copy-start(bf16[1,128,2048]{2,1,0:T(8,128)(2,1)} %param.19) | copy-start | bytes 1572868
  7.2 10.8 %copy-start.3 = (s32[1,128]{1,0:T(1,128)S(1)}, s32[1,128]{1,0:T(1,128)}, u32[]{:S(2)}) copy-start(s32[1,128]{1,0:T(1,128)} %param.15) | copy-start | bytes 1540
  7.2 77.4 %all-reduce.4.cloned.1.call-start = ((), (), s32[]{:S(2)}) async-start(), calls=%async_computation | async-start | bytes 524288 | tf_op jit(solution)/shard_map/psum | solution.py:16
  13.2 124.6 %all-gather.5.cloned.1.call-start = ((), (), s32[]{:S(2)}) async-start(), calls=%async_computation.1 | async-start | bytes 2359296 | tf_op jit(solution)/shard_map/all_gather | solution.py:97
  140.6 1.8 copy-start
  143.9 1.0 copy-start.1
Sparse Core Ops, SparseCore 0:
  13.3 71.2 all-reduce.3
  87.2 50.5 all-gather.4
where the time goes:
time: 223 us
  waiting for transfers between devices  96.5 us (43%)
  blocking collectives  79.4 us (36%)
  between operations  16.8 us (8%)
  local copies, waits for them, and re-layouts  16.4 us (7%)
  other arithmetic  7.1 us (3%)
  matrix products  4.92 us (2%)
    psum x1, waiting for transfers between devices, spread(): return lax.psum(kept, axis)  48.7 us
    all_gather x1, waiting for transfers between devices, shards(): stacked = lax.all_gather(own_pair, 'seq', axis=1, tiled=True)  47.8 us
    psum x1, blocking collectives, shards(): key_sum, value_sum = lax.psum((key_part, value_part), 'seq')  40.1 us
    all_gather x1, blocking collectives, shards(): all_segments = lax.all_gather(segments[0], 'seq', axis=0, tiled=True)  17.9 us
    all_gather x1, blocking collectives, shards(): lax.all_gather(value_sum[None].astype(jnp.bfloat16), 'dp', axis=0, tiled=...  14.2 us
    unnamed x15, local copies, waits for them, and re-layouts  7.72 us
    all_gather x1, blocking collectives, shards(): lax.all_gather(key_sum[None].astype(jnp.bfloat16), 'dp', axis=0, tiled=True)  7.3 us
  transfers between devices with their start and end apart: 2, of which 2 were waited for; matrix products, arithmetic and copies ran while one was open for 5% of the time, Pallas kernels for 0%

commit v1 on v0

v1 whole, which is shorter than its diff:
```python
import functools
import math

import jax
import jax.numpy as jnp
from jax import lax
from jax.experimental import pallas as pl
from jax.experimental.pallas import tpu as pltpu
from jax.sharding import PartitionSpec as P

KVH = 4
GROUP = 4
HD = 128
PROMPT = 128
SLOTS = 2 * KVH


def dot_nt(a, b):
    return lax.dot_general(a, b, (((1,), (1,)), ((), ())), preferred_element_type=jnp.float32)


def dot_tn(a, b):
    return lax.dot_general(a, b, (((0,), (0,)), ((), ())), preferred_element_type=jnp.float32)


def dot_nn(a, b):
    return lax.dot_general(a, b, (((1,), (0,)), ((), ())), preferred_element_type=jnp.float32)


def head_cols(c):
    return slice(c * HD, (c + 1) * HD)


def kernel(
    n, n_dp, task_ref, q_ref, k_ref, v_ref, seg_ref, pk_ref, pv_ref, g_ref,
    att_ref, kg_ref, vg_ref,
    kv, segs, sel, prs, pp, part, grs, gath, m_ref, l_ref, acc_ref,
    seg_s, seg_r, prs_s, prs_r, pag_s, pag_r, z_s, z_r, x_s, x_r,
    grs_s, grs_r, gag_s, gag_r, y_s, y_r, c_s, c_r,
):
    tok = q_ref.shape[0]
    bank = pk_ref.shape[0]
    rows = SLOTS * PROMPT // n
    n_hi = n // 2
    n_dh = n_dp // 2
    scale = 1.0 / math.sqrt(HD)
    me = lax.axis_index("seq")
    dp = lax.axis_index("dp")
    hi, lo = me // 2, me % 2
    dh, dl = dp // 2, dp % 2

    def remote(src, dst, s_sem, r_sem, to_dp, to_seq):
        return pltpu.make_async_remote_copy(
            src_ref=src, dst_ref=dst, send_sem=s_sem, recv_sem=r_sem,
            device_id=(to_dp, to_seq), device_id_type=pl.DeviceIdType.MESH,
        )

    def other(d, base, count):
        return lax.rem(base + d, count)

    def chunk(ref, j):
        return ref.at[pl.ds(pl.multiple_of(j * rows, rows), rows)]

    barrier = pltpu.get_barrier_semaphore()

    @pl.loop(1, n)
    def _(d):
        pl.semaphore_signal(barrier, inc=1, device_id=(dp, other(d, me, n)),
                            device_id_type=pl.DeviceIdType.MESH)

    @pl.loop(1, n_dp)
    def _(d):
        pl.semaphore_signal(barrier, inc=1, device_id=(other(d, dp, n_dp), me),
                            device_id_type=pl.DeviceIdType.MESH)

    task = task_ref[dp]
    for s in range(SLOTS):
        src = pk_ref if s < KVH else pv_ref
        total = jnp.zeros((PROMPT, HD), jnp.bfloat16)
        for k in range(bank):
            hit = jnp.full((PROMPT, HD), task, jnp.int32) == me * bank + k
            total = jnp.where(hit, src[k, :, head_cols(s % KVH)], total)
        sel[s * PROMPT:(s + 1) * PROMPT, :] = total

    pl.semaphore_wait(barrier, n - 1 + n_dp - 1)

    def seg_copy(src_rank, dst_rank):
        return remote(seg_ref, segs.at[src_rank], seg_s.at[dst_rank], seg_r.at[src_rank], dp, dst_rank)

    def prs_copy(src_rank, dst_rank):
        return remote(chunk(sel, dst_rank), prs.at[src_rank], prs_s.at[dst_rank], prs_r.at[src_rank], dp, dst_rank)

    def pag_copy(src_rank, dst_rank):
        return remote(chunk(pp, src_rank), chunk(pp, src_rank), pag_s.at[dst_rank], pag_r.at[src_rank], dp, dst_rank)

    def z_copy(src, blk, j):
        return remote(src, kv.at[blk * 2 + lo, j], z_s.at[blk, j], z_r.at[blk, j], dp,
                      jnp.minimum(me + 2, n - 1 - (1 - lo)))

    def x_copy(src, blk, j, side):
        return remote(src, kv.at[blk * 2 + side, j], x_s.at[blk, j], x_r.at[blk, j], dp, me + 1 - 2 * lo)

    @pl.loop(1, n)
    def _(d):
        seg_copy(me, other(d, me, n)).start()

    own = (k_ref, v_ref)

    for j in range(2):
        @pl.when(hi + 1 < n_hi)
        def _():
            z_copy(own[j], hi, j).start()

        @pl.when(lo == 0)
        def _():
            x_copy(own[j], hi, j, lo).start()

    @pl.loop(1, n)
    def _(d):
        prs_copy(me, other(d, me, n)).start()

    def queries(c):
        return jnp.concatenate([q_ref[:, head_cols(c * GROUP + g)] for g in range(GROUP)], axis=0)

    def grads(c):
        return jnp.concatenate([g_ref[:, head_cols(c * GROUP + g)] for g in range(GROUP)], axis=0)

    def wide(mask):
        return jnp.concatenate([mask] * GROUP, axis=1)

    q_seg = seg_ref[...]

    def column(row):
        return jnp.transpose(jnp.broadcast_to(row, (tok, tok)))

    def absorb(key_block, value_block, mask, first=False):
        mask = wide(mask)
        for c in range(KVH):
            st = dot_nt(key_block[:, head_cols(c)], queries(c)) * scale
            st = jnp.where(mask, st, -jnp.inf)
            peak = jnp.max(st, axis=0, keepdims=True)
            if not first:
                old = m_ref[c]
                peak = jnp.maximum(old, peak)
                shrink = jnp.exp(old - peak)
            w = jnp.exp(st - peak)
            total = jnp.sum(w, axis=0, keepdims=True)
            acc = dot_tn(value_block[:, head_cols(c)], w.astype(jnp.bfloat16))
            if not first:
                total = total + l_ref[c] * shrink
                acc = acc + acc_ref[c] * shrink
            m_ref[c] = peak
            l_ref[c] = total
            acc_ref[c] = acc

    order = lax.broadcasted_iota(jnp.int32, (tok, tok), 0) <= lax.broadcasted_iota(jnp.int32, (tok, tok), 1)
    absorb(k_ref, v_ref, (column(q_seg) == jnp.broadcast_to(q_seg, (tok, tok))) & order, True)

    def prs_add(d, total):
        src = other(d, me, n)
        prs_copy(src, me).wait_recv()
        return total + prs[src]

    pp[pl.ds(pl.multiple_of(me * rows, rows), rows), :] = lax.fori_loop(
        1, n, prs_add, sel[pl.ds(pl.multiple_of(me * rows, rows), rows), :])

    @pl.loop(1, n)
    def _(d):
        pag_copy(me, other(d, me, n)).start()

    @pl.loop(1, n)
    def _(d):
        seg_copy(other(d, me, n), me).wait_recv()

    def absorb_rank(rank):
        mask = column(segs[rank]) == jnp.broadcast_to(q_seg, (tok, tok))
        absorb(kv.at[rank, 0], kv.at[rank, 1], mask)

    @pl.when(lo == 1)
    def _():
        for j in range(2):
            x_copy(own[j], hi, j, 1 - lo).wait_recv()
        absorb_rank(me - 1)

    @pl.loop(1, hi + 1)
    def _(s):
        blk = hi - s
        for j in range(2):
            z_copy(own[j], blk, j).wait_recv()

            @pl.when(hi + 1 < n_hi)
            def _():
                z_copy(kv.at[blk * 2 + lo, j], blk, j).start()

            x_copy(kv.at[blk * 2 + lo, j], blk, j, lo).start()
        absorb_rank(blk * 2 + lo)
        for j in range(2):
            x_copy(own[j], blk, j, 1 - lo).wait_recv()
        absorb_rank(blk * 2 + 1 - lo)

    @pl.loop(1, n)
    def _(d):
        pag_copy(other(d, me, n), me).wait_recv()

    def grs_copy(src_rank, dst_rank):
        return remote(chunk(part, dst_rank), grs.at[src_rank], grs_s.at[dst_rank], grs_r.at[src_rank], dp, dst_rank)

    per_slot = n // SLOTS

    def send_slot(s):
        for i in range(per_slot):
            dst = s * per_slot + i

            @pl.when(me != dst)
            def _():
                grs_copy(me, dst).start()

    for c in range(KVH):
        q = queries(c)
        g = grads(c)
        pk = pp[c * PROMPT:(c + 1) * PROMPT, :]
        pv = pp[(KVH + c) * PROMPT:(KVH + c + 1) * PROMPT, :]
        r = dot_nt(pk, q) * scale
        old = m_ref[c]
        peak = jnp.maximum(old, jnp.max(r, axis=0, keepdims=True))
        shrink = jnp.exp(old - peak)
        w = jnp.exp(r - peak)
        total = jnp.sum(w, axis=0, keepdims=True) + l_ref[c] * shrink
        acc = dot_tn(pv, w.astype(jnp.bfloat16)) + acc_ref[c] * shrink
        att = jnp.transpose(acc / total).astype(jnp.bfloat16)
        for i in range(GROUP):
            att_ref[:, head_cols(c * GROUP + i)] = att[i * tok:(i + 1) * tok, :]
        delta = jnp.sum(jnp.transpose(g.astype(jnp.float32) * att.astype(jnp.float32)), axis=0, keepdims=True)
        probs = jnp.exp(r - (peak + jnp.log(total)))
        score_grad = probs * (dot_nt(pv, g) - delta)
        vp = dot_nn(probs.astype(jnp.bfloat16), g)
        kp = dot_nn(score_grad.astype(jnp.bfloat16), q) * scale
        part[c * PROMPT:(c + 1) * PROMPT, :] = kp.astype(jnp.bfloat16)
        part[(KVH + c) * PROMPT:(KVH + c + 1) * PROMPT, :] = vp.astype(jnp.bfloat16)
        send_slot(c)
        send_slot(KVH + c)

    def grs_add(d, total):
        src = other(d, me, n)
        grs_copy(src, me).wait_recv()
        return total + grs[src].astype(jnp.float32)

    mine = pl.ds(pl.multiple_of(me * rows, rows), rows)
    gath[dp, mine, :] = lax.fori_loop(1, n, grs_add, part[mine, :].astype(jnp.float32)).astype(jnp.bfloat16)

    def piece(b, j):
        return gath.at[b, pl.ds(pl.multiple_of(j * rows, rows), rows)]

    def gag_copy(src_rank, dst_rank):
        return remote(piece(dp, src_rank), piece(dp, src_rank), gag_s.at[dst_rank], gag_r.at[src_rank], dp, dst_rank)

    def y_copy(src_h, dst_h, j):
        b = src_h * 2 + dl
        return remote(piece(b, j), piece(b, j), y_s.at[dst_h, j], y_r.at[src_h, j], dst_h * 2 + dl, me)

    def c_copy(h, side, j):
        b = h * 2 + side
        return remote(piece(b, j), piece(b, j), c_s.at[h, j], c_r.at[h, j], dh * 2 + 1 - dl, me)

    @pl.loop(1, n)
    def _(d):
        gag_copy(me, other(d, me, n)).start()

    def pass_on(j):
        @pl.loop(1, n_dh)
        def _(e):
            y_copy(dh, other(e, dh, n_dh), j).start()
        c_copy(dh, dl, j).start()

    pass_on(me)

    @pl.loop(1, n)
    def _(d):
        src = other(d, me, n)
        gag_copy(src, me).wait_recv()
        pass_on(src)

    @pl.loop(0, n)
    def _(d):
        src = other(d, me, n)

        @pl.loop(1, n_dh)
        def _(e):
            h = other(e, dh, n_dh)
            y_copy(h, dh, src).wait_recv()
            c_copy(h, dl, src).start()

    @pl.loop(0, n)
    def _(d):
        src = other(d, me, n)

        @pl.loop(0, n_dh)
        def _(h):
            c_copy(h, 1 - dl, src).wait_recv()

    for s in range(SLOTS):
        dst = kg_ref if s < KVH else vg_ref
        for k in range(bank):
            total = jnp.zeros((PROMPT, HD), jnp.float32)
            for b in range(n_dp):
                hit = jnp.full((PROMPT, HD), task_ref[b], jnp.int32) == me * bank + k
                total = total + jnp.where(
                    hit, gath[b, s * PROMPT:(s + 1) * PROMPT, :].astype(jnp.float32), 0.0)
            dst[k, :, head_cols(s % KVH)] = total

    @pl.loop(1, n)
    def _(d):
        dst = other(d, me, n)
        seg_copy(me, dst).wait_send()
        prs_copy(me, dst).wait_send()
        pag_copy(me, dst).wait_send()
        grs_copy(me, dst).wait_send()
        gag_copy(me, dst).wait_send()

    for j in range(2):
        @pl.when(lo == 0)
        def _():
            x_copy(own[j], hi, j, lo).wait_send()

        @pl.loop(0, hi)
        def _(blk):
            x_copy(own[j], blk, j, lo).wait_send()

        @pl.when(hi + 1 < n_hi)
        def _():
            @pl.loop(0, hi + 1)
            def _(blk):
                z_copy(own[j], blk, j).wait_send()

    @pl.loop(0, n)
    def _(j):
        @pl.loop(1, n_dh)
        def _(e):
            y_copy(dh, other(e, dh, n_dh), j).wait_send()

        @pl.loop(0, n_dh)
        def _(h):
            c_copy(h, dl, j).wait_send()


def shards(n, n_dp, queries, keys, values, segments, task_ids, prompt_keys, prompt_values, grad_out):
    tok = queries.shape[1]
    width = KVH * HD
    rows = SLOTS * PROMPT // n
    bank = prompt_keys.shape[0]
    bf16, f32 = jnp.bfloat16, jnp.float32
    dma = pltpu.SemaphoreType.DMA
    vmem = pl.BlockSpec(memory_space=pltpu.VMEM)
    att, kg, vg = pl.pallas_call(
        functools.partial(kernel, n, n_dp),
        out_shape=(
            jax.ShapeDtypeStruct((tok, KVH * GROUP * HD), bf16),
            jax.ShapeDtypeStruct((bank, PROMPT, width), f32),
            jax.ShapeDtypeStruct((bank, PROMPT, width), f32),
        ),
        in_specs=[pl.BlockSpec(memory_space=pltpu.SMEM)] + [vmem] * 7,
        out_specs=(vmem, vmem, vmem),
        scratch_shapes=[
            pltpu.VMEM((n, 2, tok, width), bf16),
            pltpu.VMEM((n, 1, tok), jnp.int32),
            pltpu.VMEM((SLOTS * PROMPT, HD), bf16),
            pltpu.VMEM((n, rows, HD), bf16),
            pltpu.VMEM((SLOTS * PROMPT, HD), bf16),
            pltpu.VMEM((SLOTS * PROMPT, HD), bf16),
            pltpu.VMEM((n, rows, HD), bf16),
            pltpu.VMEM((n_dp, SLOTS * PROMPT, HD), bf16),
            pltpu.VMEM((KVH, 1, GROUP * tok), f32),
            pltpu.VMEM((KVH, 1, GROUP * tok), f32),
            pltpu.VMEM((KVH, HD, GROUP * tok), f32),
            dma((n,)), dma((n,)), dma((n,)), dma((n,)), dma((n,)), dma((n,)),
            dma((n // 2, 2)), dma((n // 2, 2)), dma((n // 2, 2)), dma((n // 2, 2)),
            dma((n,)), dma((n,)), dma((n,)), dma((n,)),
            dma((n_dp // 2, n)), dma((n_dp // 2, n)), dma((n_dp // 2, n)), dma((n_dp // 2, n)),
        ],
        compiler_params=pltpu.CompilerParams(collective_id=0, has_side_effects=True),
    )(task_ids, queries[0], keys[0], values[0], segments, prompt_keys, prompt_values, grad_out[0])
    return att[None], kg, vg


def solution(mesh):
    n, n_dp = mesh.shape["seq"], mesh.shape["dp"]
    in_specs = (
        P("dp", "seq", None),
        P("dp", "seq", None),
        P("dp", "seq", None),
        P("dp", "seq"),
        P(),
        P("seq", None, None),
        P("seq", None, None),
        P("dp", "seq", None),
    )
    out_specs = (P("dp", "seq", None), P("seq", None, None), P("seq", None, None))
    return jax.shard_map(
        functools.partial(shards, n, n_dp), mesh=mesh, in_specs=in_specs, out_specs=out_specs, check_vma=False
    )
```

time: 223 us -> 76.6 us (0.34)
  waiting for transfers between devices: 96.5 us -> 0 us
  blocking collectives: 79.4 us -> 0 us
  Pallas kernels: 0 us -> 71.8 us
  between operations: 16.8 us -> 0.65 us
  local copies, waits for them, and re-layouts: 16.4 us -> 3.97 us
  other arithmetic: 7.1 us -> 0 us
  matrix products: 4.92 us -> 0 us
    pallas_call x0 -> x1, Pallas kernels: none -> 71.8 us  [shards(): pl.pallas_call(functools.partial(kernel, n, n_dp), out_shape=(jax.ShapeDt...]
    psum x1 -> x0, waiting for transfers between devices: 48.7 us -> none  [spread(): return lax.psum(kept, axis)]
    all_gather x1 -> x0, waiting for transfers between devices: 47.8 us -> none  [shards(): stacked = lax.all_gather(own_pair, 'seq', axis=1, tiled=True)]
    psum x1 -> x0, blocking collectives: 40.1 us -> none  [shards(): key_sum, value_sum = lax.psum((key_part, value_part), 'seq')]
    all_gather x3 -> x0, blocking collectives: 39.3 us -> none  [the longest x1 17.9 us: shards(): all_segments = lax.all_gather(segments[0], 'seq', axis=0, tiled=True)]
    dot_general x6 -> x0, matrix products: 4.92 us -> none  [the longest x1 1.51 us: update(): jnp.einsum('tkgs,skd->tkgd', block_weights.astype(jnp.bfloat16), value_he...]
    unnamed x15 -> x7, local copies, waits for them, and re-layouts: 7.72 us -> 3.97 us
    while x1 -> x0, local copies, waits for them, and re-layouts: 2.55 us -> none  [shards(): carried = lax.fori_loop(0, key_count // tile_rows, loop_tile, carried)]
  transfers between devices with their start and end apart: 2 -> 0, of which waited for: 2 -> 0; matrix products, arithmetic and copies ran while one was open for 5% -> 0% of each run, Pallas kernels for 0% -> 0%
where the time goes in v1:
time: 76.6 us; the launch traced here: 76.4 us
  Pallas kernels  71.8 us (94%)
  local copies, waits for them, and re-layouts  3.97 us (5%)
    pallas_call x1, Pallas kernels, shards(): pl.pallas_call(functools.partial(kernel, n, n_dp), out_shape=(jax.ShapeDt...  71.8 us
    unnamed x7, local copies, waits for them, and re-layouts  3.97 us

profile of v1, /device:TPU:1, one launch (start us, length us, event | category | flops | bytes accessed | tf_op | source)
XLA Modules:
  0.0 76.4 jit_solution(18356699311386684737)
XLA Ops:
  0.6 71.8 %shard_map.103 = (bf16[128,2048]{1,0:T(8,128)(2,1)}, f32[2,128,512]{2,1,0:T(8,128)}, f32[2,128,512]{2,1,0:T(8,128)}) custom-call(s32[4]{0:T(128)} %task_ref.1, bf16[128,2048]{1,0:T(8,128)(2,1)} %bitcast.5, bf16[128,512]{1,0:T(8,128)(2,1)} %bitcast.8, bf16[128,512]{1,0:T(8,128)(2,1)} %bitcast.9, s32[1,128]{1,0:T(1,128)} %seg_ref.1, ...), custom_call_target="tpu_custom_call" | custom-call | tf_op jit(solution)/shard_map/pallas_call | solution.py:354
  72.4 0.0 copy-start.1
  72.4 1.9 %copy.14 = bf16[1,128,2048]{2,1,0:T(8,128)(2,1)} copy(bf16[1,128,2048]{2,1,0:T(8,128)(2,1)} %bitcast.7) | data formatting | bytes 1048576
  74.4 0.0 copy-done.1
  74.4 0.0 copy-start
  74.4 0.8 %copy.15 = f32[2,128,512]{2,1,0:T(8,128)} copy(f32[2,128,512]{2,1,0:T(8,128)S(1)} %copy-done.1) | data formatting | bytes 1048576
  75.2 0.4 copy-done
  75.6 0.8 %copy.16 = f32[2,128,512]{2,1,0:T(8,128)} copy(f32[2,128,512]{2,1,0:T(8,128)S(1)} %copy-done) | data formatting | bytes 1048576
Async XLA Ops:
  72.4 2.0 %copy-start.1 = (f32[2,128,512]{2,1,0:T(8,128)S(1)}, f32[2,128,512]{2,1,0:T(8,128)}, u32[]{:S(2)}) copy-start(f32[2,128,512]{2,1,0:T(8,128)} %get-tuple-element.13) | copy-start | bytes 1572868
  74.4 1.2 %copy-start = (f32[2,128,512]{2,1,0:T(8,128)S(1)}, f32[2,128,512]{2,1,0:T(8,128)}, u32[]{:S(2)}) copy-start(f32[2,128,512]{2,1,0:T(8,128)} %get-tuple-element.14) | copy-start | bytes 1572868

commit v2 on v1

--- a/solution.py
+++ b/solution.py
@@ -32,12 +32,19 @@
 
 
 def kernel(
-    n, n_dp, task_ref, q_ref, k_ref, v_ref, seg_ref, pk_ref, pv_ref, g_ref,
-    att_ref, kg_ref, vg_ref,
+    n, n_dp, task_ref, *refs,
+):
+    inputs, refs = refs[:7], refs[7:]
+    att_ref, kg_ref, vg_ref, held, load_s, *refs = refs
+    (
     kv, segs, sel, prs, pp, part, grs, gath, m_ref, l_ref, acc_ref,
     seg_s, seg_r, prs_s, prs_r, pag_s, pag_r, z_s, z_r, x_s, x_r,
     grs_s, grs_r, gag_s, gag_r, y_s, y_r, c_s, c_r,
-):
+    ) = refs
+    q_ref, k_ref, v_ref, seg_ref, pk_ref, pv_ref, g_ref = held
+    loads = [pltpu.make_async_copy(src, dst, load_s.at[i]) for i, (src, dst) in enumerate(zip(inputs, held))]
+    for i in (4, 5, 3, 1, 2, 0, 6):
+        loads[i].start()
     tok = q_ref.shape[0]
     bank = pk_ref.shape[0]
     rows = SLOTS * PROMPT // n
@@ -73,6 +80,9 @@
         pl.semaphore_signal(barrier, inc=1, device_id=(other(d, dp, n_dp), me),
                             device_id_type=pl.DeviceIdType.MESH)
 
+    for i in (4, 5):
+        loads[i].wait()
+
     task = task_ref[dp]
     for s in range(SLOTS):
         src = pk_ref if s < KVH else pv_ref
@@ -82,6 +92,8 @@
             total = jnp.where(hit, src[k, :, head_cols(s % KVH)], total)
         sel[s * PROMPT:(s + 1) * PROMPT, :] = total
 
+    for i in (3, 1, 2):
+        loads[i].wait()
     pl.semaphore_wait(barrier, n - 1 + n_dp - 1)
 
     def seg_copy(src_rank, dst_rank):
@@ -103,6 +115,10 @@
     @pl.loop(1, n)
     def _(d):
         seg_copy(me, other(d, me, n)).start()
+
+    @pl.loop(1, n)
+    def _(d):
+        prs_copy(me, other(d, me, n)).start()
 
     own = (k_ref, v_ref)
 
@@ -115,10 +131,6 @@
         def _():
             x_copy(own[j], hi, j, lo).start()
 
-    @pl.loop(1, n)
-    def _(d):
-        prs_copy(me, other(d, me, n)).start()
-
     def queries(c):
         return jnp.concatenate([q_ref[:, head_cols(c * GROUP + g)] for g in range(GROUP)], axis=0)
 
@@ -128,6 +140,7 @@
     def wide(mask):
         return jnp.concatenate([mask] * GROUP, axis=1)
 
+    loads[0].wait()
     q_seg = seg_ref[...]
 
     def column(row):
@@ -156,17 +169,20 @@
     order = lax.broadcasted_iota(jnp.int32, (tok, tok), 0) <= lax.broadcasted_iota(jnp.int32, (tok, tok), 1)
     absorb(k_ref, v_ref, (column(q_seg) == jnp.broadcast_to(q_seg, (tok, tok))) & order, True)
 
-    def prs_add(d, total):
-        src = other(d, me, n)
-        prs_copy(src, me).wait_recv()
-        return total + prs[src]
-
-    pp[pl.ds(pl.multiple_of(me * rows, rows), rows), :] = lax.fori_loop(
-        1, n, prs_add, sel[pl.ds(pl.multiple_of(me * rows, rows), rows), :])
-
-    @pl.loop(1, n)
-    def _(d):
-        pag_copy(me, other(d, me, n)).start()
+    def spread_prompt():
+        def prs_add(d, total):
+            src = other(d, me, n)
+            prs_copy(src, me).wait_recv()
+            return total + prs[src]
+
+        mine = pl.ds(pl.multiple_of(me * rows, rows), rows)
+        pp[mine, :] = lax.fori_loop(1, n, prs_add, sel[mine, :])
+
+        @pl.loop(1, n)
+        def _(d):
+            pag_copy(me, other(d, me, n)).start()
+
+    pl.when(hi == 0)(spread_prompt)
 
     @pl.loop(1, n)
     def _(d):
@@ -176,11 +192,10 @@
         mask = column(segs[rank]) == jnp.broadcast_to(q_seg, (tok, tok))
         absorb(kv.at[rank, 0], kv.at[rank, 1], mask)
 
-    @pl.when(lo == 1)
-    def _():
+    def absorb_crossed(blk):
         for j in range(2):
-            x_copy(own[j], hi, j, 1 - lo).wait_recv()
-        absorb_rank(me - 1)
+            x_copy(own[j], blk, j, 1 - lo).wait_recv()
+        absorb_rank(blk * 2 + 1 - lo)
 
     @pl.loop(1, hi + 1)
     def _(s):
@@ -193,14 +208,22 @@
                 z_copy(kv.at[blk * 2 + lo, j], blk, j).start()
 
             x_copy(kv.at[blk * 2 + lo, j], blk, j, lo).start()
+        pl.when(s == 1)(spread_prompt)
         absorb_rank(blk * 2 + lo)
-        for j in range(2):
-            x_copy(own[j], blk, j, 1 - lo).wait_recv()
-        absorb_rank(blk * 2 + 1 - lo)
+
+        @pl.when(jnp.logical_or(s > 1, lo == 1))
+        def _():
+            absorb_crossed(blk + 1)
+
+    @pl.when(jnp.logical_or(hi > 0, lo == 1))
+    def _():
+        absorb_crossed(0)
 
     @pl.loop(1, n)
     def _(d):
         pag_copy(other(d, me, n), me).wait_recv()
+
+    loads[6].wait()
 
     def grs_copy(src_rank, dst_rank):
         return remote(chunk(part, dst_rank), grs.at[src_rank], grs_s.at[dst_rank], grs_r.at[src_rank], dp, dst_rank)
@@ -351,6 +374,7 @@
     bf16, f32 = jnp.bfloat16, jnp.float32
     dma = pltpu.SemaphoreType.DMA
     vmem = pl.BlockSpec(memory_space=pltpu.VMEM)
+    operands = (queries[0], keys[0], values[0], segments, prompt_keys, prompt_values, grad_out[0])
     att, kg, vg = pl.pallas_call(
         functools.partial(kernel, n, n_dp),
         out_shape=(
@@ -358,9 +382,11 @@
             jax.ShapeDtypeStruct((bank, PROMPT, width), f32),
             jax.ShapeDtypeStruct((bank, PROMPT, width), f32),
         ),
-        in_specs=[pl.BlockSpec(memory_space=pltpu.SMEM)] + [vmem] * 7,
+        in_specs=[pl.BlockSpec(memory_space=pltpu.SMEM)] + [pl.BlockSpec(memory_space=pl.ANY)] * 7,
         out_specs=(vmem, vmem, vmem),
         scratch_shapes=[
+            [pltpu.VMEM(a.shape, a.dtype) for a in operands],
+            dma((7,)),
             pltpu.VMEM((n, 2, tok, width), bf16),
             pltpu.VMEM((n, 1, tok), jnp.int32),
             pltpu.VMEM((SLOTS * PROMPT, HD), bf16),
@@ -378,7 +404,7 @@
             dma((n_dp // 2, n)), dma((n_dp // 2, n)), dma((n_dp // 2, n)), dma((n_dp // 2, n)),
         ],
         compiler_params=pltpu.CompilerParams(collective_id=0, has_side_effects=True),
-    )(task_ids, queries[0], keys[0], values[0], segments, prompt_keys, prompt_values, grad_out[0])
+    )(task_ids, *operands)
     return att[None], kg, vg
 
 

time: 76.6 us -> 68.7 us (0.90)
  Pallas kernels: 71.8 us -> 63.9 us
    pallas_call x1, Pallas kernels: 71.8 us -> 63.9 us  [shards(): pl.pallas_call(functools.partial(kernel, n, n_dp), out_shape=(jax.ShapeDt...]
where the time goes in v2:
time: 68.7 us; the launch traced here: 68.5 us
  Pallas kernels  63.9 us (93%)
  local copies, waits for them, and re-layouts  3.97 us (6%)
    pallas_call x1, Pallas kernels, shards(): pl.pallas_call(functools.partial(kernel, n, n_dp), out_shape=(jax.ShapeDt...  63.9 us
    unnamed x7, local copies, waits for them, and re-layouts  3.97 us

profile of v2, /device:TPU:1, one launch (start us, length us, event | category | flops | bytes accessed | tf_op | source)
XLA Modules:
  0.0 68.5 jit_solution(6847327440034724547)
XLA Ops:
  0.6 63.9 %shard_map.103 = (bf16[128,2048]{1,0:T(8,128)(2,1)}, f32[2,128,512]{2,1,0:T(8,128)}, f32[2,128,512]{2,1,0:T(8,128)}) custom-call(s32[4]{0:T(128)} %task_ref.1, bf16[128,2048]{1,0:T(8,128)(2,1)} %bitcast.5, bf16[128,512]{1,0:T(8,128)(2,1)} %bitcast.8, bf16[128,512]{1,0:T(8,128)(2,1)} %bitcast.9, s32[1,128]{1,0:T(1,128)} %refs_3_.1, ...), custom_call_target="tpu_custom_call" | custom-call | tf_op jit(solution)/shard_map/pallas_call | solution.py:378
  64.5 0.0 copy-start.1
  64.6 1.9 %copy.14 = bf16[1,128,2048]{2,1,0:T(8,128)(2,1)} copy(bf16[1,128,2048]{2,1,0:T(8,128)(2,1)} %bitcast.7) | data formatting | bytes 1048576
  66.5 0.0 copy-done.1
  66.5 0.0 copy-start
  66.5 0.8 %copy.15 = f32[2,128,512]{2,1,0:T(8,128)} copy(f32[2,128,512]{2,1,0:T(8,128)S(1)} %copy-done.1) | data formatting | bytes 1048576
  67.3 0.4 copy-done
  67.7 0.8 %copy.16 = f32[2,128,512]{2,1,0:T(8,128)} copy(f32[2,128,512]{2,1,0:T(8,128)S(1)} %copy-done) | data formatting | bytes 1048576
Async XLA Ops:
  64.5 2.0 %copy-start.1 = (f32[2,128,512]{2,1,0:T(8,128)S(1)}, f32[2,128,512]{2,1,0:T(8,128)}, u32[]{:S(2)}) copy-start(f32[2,128,512]{2,1,0:T(8,128)} %get-tuple-element.13) | copy-start | bytes 1572868
  66.5 1.2 %copy-start = (f32[2,128,512]{2,1,0:T(8,128)S(1)}, f32[2,128,512]{2,1,0:T(8,128)}, u32[]{:S(2)}) copy-start(f32[2,128,512]{2,1,0:T(8,128)} %get-tuple-element.14) | copy-start | bytes 1572868

commit v3 on v2

--- a/solution.py
+++ b/solution.py
@@ -35,9 +35,9 @@
     n, n_dp, task_ref, *refs,
 ):
     inputs, refs = refs[:7], refs[7:]
-    att_ref, kg_ref, vg_ref, held, load_s, *refs = refs
+    att_out, gath, held, load_s, att_ref, att_s, *refs = refs
     (
-    kv, segs, sel, prs, pp, part, grs, gath, m_ref, l_ref, acc_ref,
+    kv, segs, sel, prs, pp, part, grs, m_ref, l_ref, acc_ref, r_ref, d_ref,
     seg_s, seg_r, prs_s, prs_r, pag_s, pag_r, z_s, z_r, x_s, x_r,
     grs_s, grs_r, gag_s, gag_r, y_s, y_r, c_s, c_r,
     ) = refs
@@ -116,10 +116,6 @@
     def _(d):
         seg_copy(me, other(d, me, n)).start()
 
-    @pl.loop(1, n)
-    def _(d):
-        prs_copy(me, other(d, me, n)).start()
-
     own = (k_ref, v_ref)
 
     for j in range(2):
@@ -130,6 +126,10 @@
         @pl.when(lo == 0)
         def _():
             x_copy(own[j], hi, j, lo).start()
+
+    @pl.loop(1, n)
+    def _(d):
+        prs_copy(me, other(d, me, n)).start()
 
     def queries(c):
         return jnp.concatenate([q_ref[:, head_cols(c * GROUP + g)] for g in range(GROUP)], axis=0)
@@ -208,54 +208,59 @@
                 z_copy(kv.at[blk * 2 + lo, j], blk, j).start()
 
             x_copy(kv.at[blk * 2 + lo, j], blk, j, lo).start()
-        pl.when(s == 1)(spread_prompt)
+        pl.when(s == jnp.minimum(hi, 2))(spread_prompt)
         absorb_rank(blk * 2 + lo)
 
         @pl.when(jnp.logical_or(s > 1, lo == 1))
         def _():
             absorb_crossed(blk + 1)
 
-    @pl.when(jnp.logical_or(hi > 0, lo == 1))
-    def _():
-        absorb_crossed(0)
-
     @pl.loop(1, n)
     def _(d):
         pag_copy(other(d, me, n), me).wait_recv()
 
     loads[6].wait()
-
-    def grs_copy(src_rank, dst_rank):
-        return remote(chunk(part, dst_rank), grs.at[src_rank], grs_s.at[dst_rank], grs_r.at[src_rank], dp, dst_rank)
-
-    per_slot = n // SLOTS
-
-    def send_slot(s):
-        for i in range(per_slot):
-            dst = s * per_slot + i
-
-            @pl.when(me != dst)
-            def _():
-                grs_copy(me, dst).start()
-
     for c in range(KVH):
-        q = queries(c)
-        g = grads(c)
         pk = pp[c * PROMPT:(c + 1) * PROMPT, :]
         pv = pp[(KVH + c) * PROMPT:(KVH + c + 1) * PROMPT, :]
-        r = dot_nt(pk, q) * scale
+        r = dot_nt(pk, queries(c)) * scale
         old = m_ref[c]
         peak = jnp.maximum(old, jnp.max(r, axis=0, keepdims=True))
         shrink = jnp.exp(old - peak)
         w = jnp.exp(r - peak)
-        total = jnp.sum(w, axis=0, keepdims=True) + l_ref[c] * shrink
-        acc = dot_tn(pv, w.astype(jnp.bfloat16)) + acc_ref[c] * shrink
-        att = jnp.transpose(acc / total).astype(jnp.bfloat16)
+        m_ref[c] = peak
+        l_ref[c] = jnp.sum(w, axis=0, keepdims=True) + l_ref[c] * shrink
+        acc_ref[c] = dot_tn(pv, w.astype(jnp.bfloat16)) + acc_ref[c] * shrink
+        r_ref[c] = r
+        d_ref[c] = dot_nt(pv, grads(c))
+
+    @pl.when(jnp.logical_or(hi > 0, lo == 1))
+    def _():
+        absorb_crossed(0)
+
+    def grs_copy(src_rank, dst_rank):
+        return remote(chunk(part, dst_rank), grs.at[src_rank], grs_s.at[dst_rank], grs_r.at[src_rank], dp, dst_rank)
+
+    per_slot = n // SLOTS
+
+    def send_slot(s):
+        for i in range(per_slot):
+            dst = s * per_slot + i
+
+            @pl.when(me != dst)
+            def _():
+                grs_copy(me, dst).start()
+
+    for c in range(KVH):
+        q = queries(c)
+        g = grads(c)
+        total = l_ref[c]
+        att = jnp.transpose(acc_ref[c] / total).astype(jnp.bfloat16)
         for i in range(GROUP):
             att_ref[:, head_cols(c * GROUP + i)] = att[i * tok:(i + 1) * tok, :]
         delta = jnp.sum(jnp.transpose(g.astype(jnp.float32) * att.astype(jnp.float32)), axis=0, keepdims=True)
-        probs = jnp.exp(r - (peak + jnp.log(total)))
-        score_grad = probs * (dot_nt(pv, g) - delta)
+        probs = jnp.exp(r_ref[c] - (m_ref[c] + jnp.log(total)))
+        score_grad = probs * (d_ref[c] - delta)
         vp = dot_nn(probs.astype(jnp.bfloat16), g)
         kp = dot_nn(score_grad.astype(jnp.bfloat16), q) * scale
         part[c * PROMPT:(c + 1) * PROMPT, :] = kp.astype(jnp.bfloat16)
@@ -263,6 +268,9 @@
         send_slot(c)
         send_slot(KVH + c)
 
+    att_copy = pltpu.make_async_copy(att_ref, att_out, att_s)
+    att_copy.start()
+
     def grs_add(d, total):
         src = other(d, me, n)
         grs_copy(src, me).wait_recv()
@@ -321,15 +329,7 @@
         def _(h):
             c_copy(h, 1 - dl, src).wait_recv()
 
-    for s in range(SLOTS):
-        dst = kg_ref if s < KVH else vg_ref
-        for k in range(bank):
-            total = jnp.zeros((PROMPT, HD), jnp.float32)
-            for b in range(n_dp):
-                hit = jnp.full((PROMPT, HD), task_ref[b], jnp.int32) == me * bank + k
-                total = total + jnp.where(
-                    hit, gath[b, s * PROMPT:(s + 1) * PROMPT, :].astype(jnp.float32), 0.0)
-            dst[k, :, head_cols(s % KVH)] = total
+    att_copy.wait()
 
     @pl.loop(1, n)
     def _(d):
@@ -364,6 +364,41 @@
         @pl.loop(0, n_dh)
         def _(h):
             c_copy(h, dl, j).wait_send()
+
+
+def finish(n_dp, task_ref, att_in, gath_in, att_out, kg_out, vg_out, att_v, gath_v, kg_v, vg_v, sems, out_s):
+    bank = kg_v.shape[0]
+    me = lax.axis_index("seq")
+    att_load = pltpu.make_async_copy(att_in, att_v, sems.at[SLOTS])
+    att_store = pltpu.make_async_copy(att_v, att_out, out_s.at[2 * bank])
+
+    def load(s):
+        rows = pl.ds(s * PROMPT, PROMPT)
+        return pltpu.make_async_copy(gath_in.at[:, rows], gath_v.at[:, rows], sems.at[s])
+
+    for s in range(SLOTS):
+        load(s).start()
+        if s == 1:
+            att_load.start()
+    stores = [att_store]
+    for s in range(SLOTS):
+        load(s).wait()
+        held, out = (kg_v, kg_out) if s < KVH else (vg_v, vg_out)
+        for k in range(bank):
+            total = jnp.zeros((PROMPT, HD), jnp.float32)
+            for b in range(n_dp):
+                hit = jnp.full((PROMPT, HD), task_ref[b], jnp.int32) == me * bank + k
+                total = total + jnp.where(
+                    hit, gath_v[b, s * PROMPT:(s + 1) * PROMPT, :].astype(jnp.float32), 0.0)
+            held[k, :, head_cols(s % KVH)] = total
+            if s % KVH == KVH - 1:
+                stores.append(pltpu.make_async_copy(held.at[k], out.at[k], out_s.at[s // KVH * bank + k]))
+                stores[-1].start()
+        if s == 2:
+            att_load.wait()
+            att_store.start()
+    for store in stores:
+        store.wait()
 
 
 def shards(n, n_dp, queries, keys, values, segments, task_ids, prompt_keys, prompt_values, grad_out):
@@ -375,18 +410,19 @@
     dma = pltpu.SemaphoreType.DMA
     vmem = pl.BlockSpec(memory_space=pltpu.VMEM)
     operands = (queries[0], keys[0], values[0], segments, prompt_keys, prompt_values, grad_out[0])
-    att, kg, vg = pl.pallas_call(
+    att, gath = pl.pallas_call(
         functools.partial(kernel, n, n_dp),
         out_shape=(
             jax.ShapeDtypeStruct((tok, KVH * GROUP * HD), bf16),
-            jax.ShapeDtypeStruct((bank, PROMPT, width), f32),
-            jax.ShapeDtypeStruct((bank, PROMPT, width), f32),
+            jax.ShapeDtypeStruct((n_dp, SLOTS * PROMPT, HD), bf16),
         ),
         in_specs=[pl.BlockSpec(memory_space=pltpu.SMEM)] + [pl.BlockSpec(memory_space=pl.ANY)] * 7,
-        out_specs=(vmem, vmem, vmem),
+        out_specs=(pl.BlockSpec(memory_space=pl.ANY), vmem),
         scratch_shapes=[
             [pltpu.VMEM(a.shape, a.dtype) for a in operands],
             dma((7,)),
+            pltpu.VMEM((tok, KVH * GROUP * HD), bf16),
+            dma,
             pltpu.VMEM((n, 2, tok, width), bf16),
             pltpu.VMEM((n, 1, tok), jnp.int32),
             pltpu.VMEM((SLOTS * PROMPT, HD), bf16),
@@ -394,10 +430,11 @@
             pltpu.VMEM((SLOTS * PROMPT, HD), bf16),
             pltpu.VMEM((SLOTS * PROMPT, HD), bf16),
             pltpu.VMEM((n, rows, HD), bf16),
-            pltpu.VMEM((n_dp, SLOTS * PROMPT, HD), bf16),
             pltpu.VMEM((KVH, 1, GROUP * tok), f32),
             pltpu.VMEM((KVH, 1, GROUP * tok), f32),
             pltpu.VMEM((KVH, HD, GROUP * tok), f32),
+            pltpu.VMEM((KVH, PROMPT, GROUP * tok), f32),
+            pltpu.VMEM((KVH, PROMPT, GROUP * tok), f32),
             dma((n,)), dma((n,)), dma((n,)), dma((n,)), dma((n,)), dma((n,)),
             dma((n // 2, 2)), dma((n // 2, 2)), dma((n // 2, 2)), dma((n // 2, 2)),
             dma((n,)), dma((n,)), dma((n,)), dma((n,)),
@@ -405,6 +442,25 @@
         ],
         compiler_params=pltpu.CompilerParams(collective_id=0, has_side_effects=True),
     )(task_ids, *operands)
+    anyspace = pl.BlockSpec(memory_space=pl.ANY)
+    att, kg, vg = pl.pallas_call(
+        functools.partial(finish, n_dp),
+        out_shape=(
+            jax.ShapeDtypeStruct((tok, KVH * GROUP * HD), bf16),
+            jax.ShapeDtypeStruct((bank, PROMPT, width), f32),
+            jax.ShapeDtypeStruct((bank, PROMPT, width), f32),
+        ),
+        in_specs=[pl.BlockSpec(memory_space=pltpu.SMEM), anyspace, anyspace],
+        out_specs=(anyspace, anyspace, anyspace),
+        scratch_shapes=[
+            pltpu.VMEM((tok, KVH * GROUP * HD), bf16),
+            pltpu.VMEM((n_dp, SLOTS * PROMPT, HD), bf16),
+            pltpu.VMEM((bank, PROMPT, width), f32),
+            pltpu.VMEM((bank, PROMPT, width), f32),
+            dma((SLOTS + 1,)),
+            dma((2 * bank + 1,)),
+        ],
+    )(task_ids, att, gath)
     return att[None], kg, vg
 
 

time: 68.7 us -> 64.5 us (0.939)
  local copies, waits for them, and re-layouts: 3.97 us -> 0 us
    unnamed x7 -> x0, local copies, waits for them, and re-layouts: 3.97 us -> none
    pallas_call x1, Pallas kernels: 63.9 us -> 60.5 us  [shards(): pl.pallas_call(functools.partial(kernel, n, n_dp), out_shape=(jax.ShapeDt...]
    pallas_call x0 -> x1, Pallas kernels: none -> 3.16 us  [shards(): pl.pallas_call(functools.partial(finish, n_dp), out_shape=(jax.ShapeDtype...]
where the time goes in v3:
time: 64.5 us; the launch traced here: 64.3 us
  Pallas kernels  63.7 us (99%)
    pallas_call x1, Pallas kernels, shards(): pl.pallas_call(functools.partial(kernel, n, n_dp), out_shape=(jax.ShapeDt...  60.5 us
    pallas_call x1, Pallas kernels, shards(): pl.pallas_call(functools.partial(finish, n_dp), out_shape=(jax.ShapeDtype...  3.16 us

profile of v3, /device:TPU:1, one launch (start us, length us, event | category | flops | bytes accessed | tf_op | source)
XLA Modules:
  0.0 64.3 jit_solution(18244498935000304661)
XLA Ops:
  0.6 60.5 %shard_map.103 = (bf16[128,2048]{1,0:T(8,128)(2,1)}, bf16[4,1024,128]{2,1,0:T(8,128)(2,1)}) custom-call(s32[4]{0:T(128)} %task_ref.3, bf16[128,2048]{1,0:T(8,128)(2,1)} %bitcast.5, bf16[128,512]{1,0:T(8,128)(2,1)} %bitcast.7, bf16[128,512]{1,0:T(8,128)(2,1)} %bitcast.8, s32[1,128]{1,0:T(1,128)} %refs_3_.1, bf16[2,128,512]{2,1,0:T(8,128)(2,1)} %refs_4_.1, ...), custom_call_target="tpu_custom_call" | custom-call | tf_op jit(solution)/shard_map/pallas_call | solution.py:413
  61.2 3.2 %shard_map.104 = (bf16[128,2048]{1,0:T(8,128)(2,1)}, f32[2,128,512]{2,1,0:T(8,128)}, f32[2,128,512]{2,1,0:T(8,128)}) custom-call(s32[4]{0:T(128)} %task_ref.3, bf16[128,2048]{1,0:T(8,128)(2,1)} %get-tuple-element.8.att_in, bf16[4,1024,128]{2,1,0:T(8,128)(2,1)} %get-tuple-element.9.gath_in), custom_call_target="tpu_custom_call" | custom-call | tf_op jit(solution)/shard_map/pallas_call | solution.py:446

commit v4 on v3

--- a/solution.py
+++ b/solution.py
@@ -35,7 +35,7 @@
     n, n_dp, task_ref, *refs,
 ):
     inputs, refs = refs[:7], refs[7:]
-    att_out, gath, held, load_s, att_ref, att_s, *refs = refs
+    att_ref, gath, held, load_s, *refs = refs
     (
     kv, segs, sel, prs, pp, part, grs, m_ref, l_ref, acc_ref, r_ref, d_ref,
     seg_s, seg_r, prs_s, prs_r, pag_s, pag_r, z_s, z_r, x_s, x_r,
@@ -268,9 +268,6 @@
         send_slot(c)
         send_slot(KVH + c)
 
-    att_copy = pltpu.make_async_copy(att_ref, att_out, att_s)
-    att_copy.start()
-
     def grs_add(d, total):
         src = other(d, me, n)
         grs_copy(src, me).wait_recv()
@@ -328,8 +325,6 @@
         @pl.loop(0, n_dh)
         def _(h):
             c_copy(h, 1 - dl, src).wait_recv()
-
-    att_copy.wait()
 
     @pl.loop(1, n)
     def _(d):
@@ -366,23 +361,12 @@
             c_copy(h, dl, j).wait_send()
 
 
-def finish(n_dp, task_ref, att_in, gath_in, att_out, kg_out, vg_out, att_v, gath_v, kg_v, vg_v, sems, out_s):
+def finish(n_dp, task_ref, att_v, gath_v, att_out, kg_out, vg_out, kg_v, vg_v, out_s):
     bank = kg_v.shape[0]
     me = lax.axis_index("seq")
-    att_load = pltpu.make_async_copy(att_in, att_v, sems.at[SLOTS])
-    att_store = pltpu.make_async_copy(att_v, att_out, out_s.at[2 * bank])
-
-    def load(s):
-        rows = pl.ds(s * PROMPT, PROMPT)
-        return pltpu.make_async_copy(gath_in.at[:, rows], gath_v.at[:, rows], sems.at[s])
-
+    stores = [pltpu.make_async_copy(att_v, att_out, out_s.at[2 * bank])]
+    stores[0].start()
     for s in range(SLOTS):
-        load(s).start()
-        if s == 1:
-            att_load.start()
-    stores = [att_store]
-    for s in range(SLOTS):
-        load(s).wait()
         held, out = (kg_v, kg_out) if s < KVH else (vg_v, vg_out)
         for k in range(bank):
             total = jnp.zeros((PROMPT, HD), jnp.float32)
@@ -394,9 +378,6 @@
             if s % KVH == KVH - 1:
                 stores.append(pltpu.make_async_copy(held.at[k], out.at[k], out_s.at[s // KVH * bank + k]))
                 stores[-1].start()
-        if s == 2:
-            att_load.wait()
-            att_store.start()
     for store in stores:
         store.wait()
 
@@ -413,16 +394,14 @@
     att, gath = pl.pallas_call(
         functools.partial(kernel, n, n_dp),
         out_shape=(
-            jax.ShapeDtypeStruct((tok, KVH * GROUP * HD), bf16),
-            jax.ShapeDtypeStruct((n_dp, SLOTS * PROMPT, HD), bf16),
+            pltpu.VMEM((tok, KVH * GROUP * HD), bf16),
+            pltpu.VMEM((n_dp, SLOTS * PROMPT, HD), bf16),
         ),
         in_specs=[pl.BlockSpec(memory_space=pltpu.SMEM)] + [pl.BlockSpec(memory_space=pl.ANY)] * 7,
-        out_specs=(pl.BlockSpec(memory_space=pl.ANY), vmem),
+        out_specs=(vmem, vmem),
         scratch_shapes=[
             [pltpu.VMEM(a.shape, a.dtype) for a in operands],
             dma((7,)),
-            pltpu.VMEM((tok, KVH * GROUP * HD), bf16),
-            dma,
             pltpu.VMEM((n, 2, tok, width), bf16),
             pltpu.VMEM((n, 1, tok), jnp.int32),
             pltpu.VMEM((SLOTS * PROMPT, HD), bf16),
@@ -450,17 +429,14 @@
             jax.ShapeDtypeStruct((bank, PROMPT, width), f32),
             jax.ShapeDtypeStruct((bank, PROMPT, width), f32),
         ),
-        in_specs=[pl.BlockSpec(memory_space=pltpu.SMEM), anyspace, anyspace],
+        in_specs=[pl.BlockSpec(memory_space=pltpu.SMEM), vmem, vmem],
         out_specs=(anyspace, anyspace, anyspace),
         scratch_shapes=[
-            pltpu.VMEM((tok, KVH * GROUP * HD), bf16),
-            pltpu.VMEM((n_dp, SLOTS * PROMPT, HD), bf16),
             pltpu.VMEM((bank, PROMPT, width), f32),
             pltpu.VMEM((bank, PROMPT, width), f32),
-            dma((SLOTS + 1,)),
             dma((2 * bank + 1,)),
         ],
-    )(task_ids, att, gath)
+    )(task_ids, *[pltpu.with_memory_space_constraint(a, pltpu.VMEM) for a in (att, gath)])
     return att[None], kg, vg
 
 

time: 64.5 us -> 62.2 us (0.964)
  Pallas kernels: 63.7 us -> 61.4 us
    pallas_call x1, Pallas kernels: 3.16 us -> 1.85 us  [shards(): pl.pallas_call(functools.partial(finish, n_dp), out_shape=(jax.ShapeDtype...]
    pallas_call x1, Pallas kernels: 60.5 us -> 59.5 us  [shards(): pl.pallas_call(functools.partial(kernel, n, n_dp), out_shape=(pltpu.VMEM(...]
where the time goes in v4:
time: 62.2 us; the launch traced here: 62 us
  Pallas kernels  61.4 us (99%)
  between operations  0.64 us (1%)
    pallas_call x1, Pallas kernels, shards(): pl.pallas_call(functools.partial(kernel, n, n_dp), out_shape=(pltpu.VMEM(...  59.5 us
    pallas_call x1, Pallas kernels, shards(): pl.pallas_call(functools.partial(finish, n_dp), out_shape=(jax.ShapeDtype...  1.85 us

profile of v4, /device:TPU:1, one launch (start us, length us, event | category | flops | bytes accessed | tf_op | source)
XLA Modules:
  0.0 62.0 jit_solution(8376150074313117771)
XLA Ops:
  0.6 59.5 %shard_map.103 = (bf16[128,2048]{1,0:T(8,128)(2,1)S(1)}, bf16[4,1024,128]{2,1,0:T(8,128)(2,1)S(1)}) custom-call(s32[4]{0:T(128)} %task_ref.3, bf16[128,2048]{1,0:T(8,128)(2,1)} %bitcast.5, bf16[128,512]{1,0:T(8,128)(2,1)} %bitcast.7, bf16[128,512]{1,0:T(8,128)(2,1)} %bitcast.8, s32[1,128]{1,0:T(1,128)} %refs_3_.1, bf16[2,128,512]{2,1,0:T(8,128)(2,1)} %refs_4_.1, ...), custom_call_target="tpu_custom_call" | custom-call | tf_op jit(solution)/shard_map/pallas_call | solution.py:394
  60.2 1.9 %shard_map.104 = (bf16[128,2048]{1,0:T(8,128)(2,1)}, f32[2,128,512]{2,1,0:T(8,128)}, f32[2,128,512]{2,1,0:T(8,128)}) custom-call(s32[4]{0:T(128)} %task_ref.3, bf16[128,2048]{1,0:T(8,128)(2,1)S(1)} %get-tuple-element.8.att_v, bf16[4,1024,128]{2,1,0:T(8,128)(2,1)S(1)} %get-tuple-element.9.gath_v), custom_call_target="tpu_custom_call" | custom-call | tf_op jit(solution)/shard_map/pallas_call | solution.py:425

commit v5 on v4

--- a/solution.py
+++ b/solution.py
@@ -37,7 +37,7 @@
     inputs, refs = refs[:7], refs[7:]
     att_ref, gath, held, load_s, *refs = refs
     (
-    kv, segs, sel, prs, pp, part, grs, m_ref, l_ref, acc_ref, r_ref, d_ref,
+    kv, segs, sel, xa, mix, w_s, w_r, sw_s, sw_r, prs, pp, part, grs, m_ref, l_ref, acc_ref, r_ref, d_ref,
     seg_s, seg_r, prs_s, prs_r, pag_s, pag_r, z_s, z_r, x_s, x_r,
     grs_s, grs_r, gag_s, gag_r, y_s, y_r, c_s, c_r,
     ) = refs
@@ -99,11 +99,27 @@
     def seg_copy(src_rank, dst_rank):
         return remote(seg_ref, segs.at[src_rank], seg_s.at[dst_rank], seg_r.at[src_rank], dp, dst_rank)
 
-    def prs_copy(src_rank, dst_rank):
-        return remote(chunk(sel, dst_rank), prs.at[src_rank], prs_s.at[dst_rank], prs_r.at[src_rank], dp, dst_rank)
-
-    def pag_copy(src_rank, dst_rank):
-        return remote(chunk(pp, src_rank), chunk(pp, src_rank), pag_s.at[dst_rank], pag_r.at[src_rank], dp, dst_rank)
+    half = SLOTS * PROMPT // 2
+
+    def half_rows(side):
+        return pl.ds(pl.multiple_of(side * half, half), half)
+
+    def lane(h):
+        return h * 2 + lo
+
+    def swap_copy():
+        return remote(sel.at[half_rows(1 - lo)], xa, sw_s.at[0], sw_r.at[0], dp, me + 1 - 2 * lo)
+
+    def prs_copy(src_h, dst_h):
+        return remote(chunk(mix, dst_h), prs.at[src_h], prs_s.at[dst_h], prs_r.at[src_h], dp, lane(dst_h))
+
+    def pag_copy(src_h, dst_h):
+        here = chunk(pp, lo * n_hi + src_h)
+        return remote(here, here, pag_s.at[dst_h], pag_r.at[src_h], dp, lane(dst_h))
+
+    def back_copy(side):
+        here = pp.at[half_rows(side)]
+        return remote(here, here, sw_s.at[1], sw_r.at[1], dp, me + 1 - 2 * lo)
 
     def z_copy(src, blk, j):
         return remote(src, kv.at[blk * 2 + lo, j], z_s.at[blk, j], z_r.at[blk, j], dp,
@@ -112,10 +128,15 @@
     def x_copy(src, blk, j, side):
         return remote(src, kv.at[blk * 2 + side, j], x_s.at[blk, j], x_r.at[blk, j], dp, me + 1 - 2 * lo)
 
+    def w_copy():
+        here = kv.at[1 - lo, 1]
+        return remote(here, here, w_s.at[0], w_r.at[0], dp, jnp.minimum(me + 2, n - 1 - (1 - lo)))
+
     @pl.loop(1, n)
     def _(d):
         seg_copy(me, other(d, me, n)).start()
 
+    swap_copy().start()
     own = (k_ref, v_ref)
 
     for j in range(2):
@@ -123,13 +144,9 @@
         def _():
             z_copy(own[j], hi, j).start()
 
-        @pl.when(lo == 0)
+        @pl.when(jnp.logical_or(lo == 0, hi == 0) if j else lo == 0)
         def _():
             x_copy(own[j], hi, j, lo).start()
-
-    @pl.loop(1, n)
-    def _(d):
-        prs_copy(me, other(d, me, n)).start()
 
     def queries(c):
         return jnp.concatenate([q_ref[:, head_cols(c * GROUP + g)] for g in range(GROUP)], axis=0)
@@ -169,20 +186,41 @@
     order = lax.broadcasted_iota(jnp.int32, (tok, tok), 0) <= lax.broadcasted_iota(jnp.int32, (tok, tok), 1)
     absorb(k_ref, v_ref, (column(q_seg) == jnp.broadcast_to(q_seg, (tok, tok))) & order, True)
 
+    swap_copy().wait_recv()
+    mix[...] = sel[half_rows(lo), :] + xa[...]
+
+    @pl.loop(1, n_hi)
+    def _(d):
+        prs_copy(hi, other(d, hi, n_hi)).start()
+
     def spread_prompt():
         def prs_add(d, total):
-            src = other(d, me, n)
-            prs_copy(src, me).wait_recv()
+            src = other(d, hi, n_hi)
+            prs_copy(src, hi).wait_recv()
             return total + prs[src]
 
-        mine = pl.ds(pl.multiple_of(me * rows, rows), rows)
-        pp[mine, :] = lax.fori_loop(1, n, prs_add, sel[mine, :])
-
-        @pl.loop(1, n)
+        first = mix[pl.ds(pl.multiple_of(hi * rows, rows), rows), :]
+        pp[pl.ds(pl.multiple_of((lo * n_hi + hi) * rows, rows), rows), :] = lax.fori_loop(1, n_hi, prs_add, first)
+
+        @pl.loop(1, n_hi)
         def _(d):
-            pag_copy(me, other(d, me, n)).start()
-
-    pl.when(hi == 0)(spread_prompt)
+            pag_copy(hi, other(d, hi, n_hi)).start()
+
+    def return_prompt():
+        @pl.loop(1, n_hi)
+        def _(d):
+            pag_copy(other(d, hi, n_hi), hi).wait_recv()
+
+        back_copy(lo).start()
+
+    @pl.when(hi == 0)
+    def _():
+        x_copy(own[1], hi, 1, 1 - lo).wait_recv()
+
+        @pl.when(hi + 1 < n_hi)
+        def _():
+            w_copy().start()
+        spread_prompt()
 
     @pl.loop(1, n)
     def _(d):
@@ -200,6 +238,7 @@
     @pl.loop(1, hi + 1)
     def _(s):
         blk = hi - s
+        pl.when(jnp.logical_and(s == hi, hi >= 3))(return_prompt)
         for j in range(2):
             z_copy(own[j], blk, j).wait_recv()
 
@@ -207,7 +246,14 @@
             def _():
                 z_copy(kv.at[blk * 2 + lo, j], blk, j).start()
 
-            x_copy(kv.at[blk * 2 + lo, j], blk, j, lo).start()
+            @pl.when(blk > 0 if j else blk >= 0)
+            def _():
+                x_copy(kv.at[blk * 2 + lo, j], blk, j, lo).start()
+
+        @pl.when(jnp.logical_and(s == hi, hi + 1 < n_hi))
+        def _():
+            w_copy().wait_recv()
+            w_copy().start()
         pl.when(s == jnp.minimum(hi, 2))(spread_prompt)
         absorb_rank(blk * 2 + lo)
 
@@ -215,9 +261,8 @@
         def _():
             absorb_crossed(blk + 1)
 
-    @pl.loop(1, n)
-    def _(d):
-        pag_copy(other(d, me, n), me).wait_recv()
+    pl.when(hi < 3)(return_prompt)
+    back_copy(1 - lo).wait_recv()
 
     loads[6].wait()
     for c in range(KVH):
@@ -234,9 +279,14 @@
         r_ref[c] = r
         d_ref[c] = dot_nt(pv, grads(c))
 
+    @pl.when(jnp.logical_and(hi > 0, hi + 1 == n_hi))
+    def _():
+        w_copy().wait_recv()
+
     @pl.when(jnp.logical_or(hi > 0, lo == 1))
     def _():
-        absorb_crossed(0)
+        x_copy(own[0], 0, 0, 1 - lo).wait_recv()
+        absorb_rank(1 - lo)
 
     def grs_copy(src_rank, dst_rank):
         return remote(chunk(part, dst_rank), grs.at[src_rank], grs_s.at[dst_rank], grs_r.at[src_rank], dp, dst_rank)
@@ -330,17 +380,25 @@
     def _(d):
         dst = other(d, me, n)
         seg_copy(me, dst).wait_send()
-        prs_copy(me, dst).wait_send()
-        pag_copy(me, dst).wait_send()
         grs_copy(me, dst).wait_send()
         gag_copy(me, dst).wait_send()
 
+    swap_copy().wait_send()
+    pl.when(hi + 1 < n_hi)(lambda: w_copy().wait_send())
+    back_copy(lo).wait_send()
+
+    @pl.loop(1, n_hi)
+    def _(d):
+        dst = other(d, hi, n_hi)
+        prs_copy(hi, dst).wait_send()
+        pag_copy(hi, dst).wait_send()
+
     for j in range(2):
-        @pl.when(lo == 0)
+        @pl.when(jnp.logical_or(lo == 0, hi == 0) if j else lo == 0)
         def _():
             x_copy(own[j], hi, j, lo).wait_send()
 
-        @pl.loop(0, hi)
+        @pl.loop(j, hi)
         def _(blk):
             x_copy(own[j], blk, j, lo).wait_send()
 
@@ -405,7 +463,10 @@
             pltpu.VMEM((n, 2, tok, width), bf16),
             pltpu.VMEM((n, 1, tok), jnp.int32),
             pltpu.VMEM((SLOTS * PROMPT, HD), bf16),
-            pltpu.VMEM((n, rows, HD), bf16),
+            pltpu.VMEM((SLOTS * PROMPT // 2, HD), bf16),
+            pltpu.VMEM((SLOTS * PROMPT // 2, HD), bf16),
+            dma((1,)), dma((1,)), dma((2,)), dma((2,)),
+            pltpu.VMEM((n // 2, rows, HD), bf16),
             pltpu.VMEM((SLOTS * PROMPT, HD), bf16),
             pltpu.VMEM((SLOTS * PROMPT, HD), bf16),
             pltpu.VMEM((n, rows, HD), bf16),
@@ -414,7 +475,7 @@
             pltpu.VMEM((KVH, HD, GROUP * tok), f32),
             pltpu.VMEM((KVH, PROMPT, GROUP * tok), f32),
             pltpu.VMEM((KVH, PROMPT, GROUP * tok), f32),
-            dma((n,)), dma((n,)), dma((n,)), dma((n,)), dma((n,)), dma((n,)),
+            dma((n,)), dma((n,)), dma((n // 2,)), dma((n // 2,)), dma((n // 2,)), dma((n // 2,)),
             dma((n // 2, 2)), dma((n // 2, 2)), dma((n // 2, 2)), dma((n // 2, 2)),
             dma((n,)), dma((n,)), dma((n,)), dma((n,)),
             dma((n_dp // 2, n)), dma((n_dp // 2, n)), dma((n_dp // 2, n)), dma((n_dp // 2, n)),

time: 62.2 us -> 61.5 us (0.989)
  Pallas kernels: 61.4 us -> 60.7 us
    pallas_call x1, Pallas kernels: 59.5 us -> 58.9 us  [shards(): pl.pallas_call(functools.partial(kernel, n, n_dp), out_shape=(pltpu.VMEM(...]
where the time goes in v5:
time: 61.5 us; the launch traced here: 61.3 us
  Pallas kernels  60.7 us (99%)
  between operations  0.64 us (1%)
    pallas_call x1, Pallas kernels, shards(): pl.pallas_call(functools.partial(kernel, n, n_dp), out_shape=(pltpu.VMEM(...  58.9 us
    pallas_call x1, Pallas kernels, shards(): pl.pallas_call(functools.partial(finish, n_dp), out_shape=(jax.ShapeDtype...  1.85 us

profile of v5, /device:TPU:1, one launch (start us, length us, event | category | flops | bytes accessed | tf_op | source)
XLA Modules:
  0.0 61.3 jit_solution(5299521119197612938)
XLA Ops:
  0.6 58.9 %shard_map.103 = (bf16[128,2048]{1,0:T(8,128)(2,1)S(1)}, bf16[4,1024,128]{2,1,0:T(8,128)(2,1)S(1)}) custom-call(s32[4]{0:T(128)} %task_ref.3, bf16[128,2048]{1,0:T(8,128)(2,1)} %bitcast.5, bf16[128,512]{1,0:T(8,128)(2,1)} %bitcast.7, bf16[128,512]{1,0:T(8,128)(2,1)} %bitcast.8, s32[1,128]{1,0:T(1,128)} %refs_3_.1, bf16[2,128,512]{2,1,0:T(8,128)(2,1)} %refs_4_.1, ...), custom_call_target="tpu_custom_call" | custom-call | tf_op jit(solution)/shard_map/pallas_call | solution.py:452
  59.5 1.9 %shard_map.104 = (bf16[128,2048]{1,0:T(8,128)(2,1)}, f32[2,128,512]{2,1,0:T(8,128)}, f32[2,128,512]{2,1,0:T(8,128)}) custom-call(s32[4]{0:T(128)} %task_ref.3, bf16[128,2048]{1,0:T(8,128)(2,1)S(1)} %get-tuple-element.8.att_v, bf16[4,1024,128]{2,1,0:T(8,128)(2,1)S(1)} %get-tuple-element.9.gath_v), custom_call_target="tpu_custom_call" | custom-call | tf_op jit(solution)/shard_map/pallas_call | solution.py:486

commit v6 on v5

--- a/solution.py
+++ b/solution.py
@@ -37,7 +37,7 @@
     inputs, refs = refs[:7], refs[7:]
     att_ref, gath, held, load_s, *refs = refs
     (
-    kv, segs, sel, xa, mix, w_s, w_r, sw_s, sw_r, prs, pp, part, grs, m_ref, l_ref, acc_ref, r_ref, d_ref,
+    kv, segs, sel, near_ref, xa, mix, w_s, w_r, sw_s, sw_r, prs, pp, part, grs, m_ref, l_ref, acc_ref, r_ref, d_ref,
     seg_s, seg_r, prs_s, prs_r, pag_s, pag_r, z_s, z_r, x_s, x_r,
     grs_s, grs_r, gag_s, gag_r, y_s, y_r, c_s, c_r,
     ) = refs
@@ -163,9 +163,9 @@
     def column(row):
         return jnp.transpose(jnp.broadcast_to(row, (tok, tok)))
 
-    def absorb(key_block, value_block, mask, first=False):
+    def absorb(key_block, value_block, mask, first=False, heads=range(KVH)):
         mask = wide(mask)
-        for c in range(KVH):
+        for c in heads:
             st = dot_nt(key_block[:, head_cols(c)], queries(c)) * scale
             st = jnp.where(mask, st, -jnp.inf)
             peak = jnp.max(st, axis=0, keepdims=True)
@@ -283,10 +283,12 @@
     def _():
         w_copy().wait_recv()
 
-    @pl.when(jnp.logical_or(hi > 0, lo == 1))
+    crossed = jnp.logical_or(hi > 0, lo == 1)
+
+    @pl.when(crossed)
     def _():
+        near_ref[...] = column(segs[1 - lo])
         x_copy(own[0], 0, 0, 1 - lo).wait_recv()
-        absorb_rank(1 - lo)
 
     def grs_copy(src_rank, dst_rank):
         return remote(chunk(part, dst_rank), grs.at[src_rank], grs_s.at[dst_rank], grs_r.at[src_rank], dp, dst_rank)
@@ -302,6 +304,11 @@
                 grs_copy(me, dst).start()
 
     for c in range(KVH):
+        @pl.when(crossed)
+        def _():
+            mask = near_ref[...] == jnp.broadcast_to(q_seg, (tok, tok))
+            absorb(kv.at[1 - lo, 0], kv.at[1 - lo, 1], mask, heads=(c,))
+
         q = queries(c)
         g = grads(c)
         total = l_ref[c]
@@ -463,6 +470,7 @@
             pltpu.VMEM((n, 2, tok, width), bf16),
             pltpu.VMEM((n, 1, tok), jnp.int32),
             pltpu.VMEM((SLOTS * PROMPT, HD), bf16),
+            pltpu.VMEM((tok, tok), jnp.int32),
             pltpu.VMEM((SLOTS * PROMPT // 2, HD), bf16),
             pltpu.VMEM((SLOTS * PROMPT // 2, HD), bf16),
             dma((1,)), dma((1,)), dma((2,)), dma((2,)),

time: 61.5 us -> 60.3 us (0.980)
  Pallas kernels: 60.7 us -> 59.5 us
    pallas_call x1, Pallas kernels: 58.9 us -> 57.6 us  [shards(): pl.pallas_call(functools.partial(kernel, n, n_dp), out_shape=(pltpu.VMEM(...]
where the time goes in v6:
time: 60.3 us; the launch traced here: 60.1 us
  Pallas kernels  59.5 us (99%)
  between operations  0.64 us (1%)
    pallas_call x1, Pallas kernels, shards(): pl.pallas_call(functools.partial(kernel, n, n_dp), out_shape=(pltpu.VMEM(...  57.6 us
    pallas_call x1, Pallas kernels, shards(): pl.pallas_call(functools.partial(finish, n_dp), out_shape=(jax.ShapeDtype...  1.85 us

profile of v6, /device:TPU:1, one launch (start us, length us, event | category | flops | bytes accessed | tf_op | source)
XLA Modules:
  0.0 60.1 jit_solution(6077569864061487890)
XLA Ops:
  0.6 57.6 %shard_map.103 = (bf16[128,2048]{1,0:T(8,128)(2,1)S(1)}, bf16[4,1024,128]{2,1,0:T(8,128)(2,1)S(1)}) custom-call(s32[4]{0:T(128)} %task_ref.3, bf16[128,2048]{1,0:T(8,128)(2,1)} %bitcast.5, bf16[128,512]{1,0:T(8,128)(2,1)} %bitcast.7, bf16[128,512]{1,0:T(8,128)(2,1)} %bitcast.8, s32[1,128]{1,0:T(1,128)} %refs_3_.1, bf16[2,128,512]{2,1,0:T(8,128)(2,1)} %refs_4_.1, ...), custom_call_target="tpu_custom_call" | custom-call | tf_op jit(solution)/shard_map/pallas_call | solution.py:459
  58.2 1.9 %shard_map.104 = (bf16[128,2048]{1,0:T(8,128)(2,1)}, f32[2,128,512]{2,1,0:T(8,128)}, f32[2,128,512]{2,1,0:T(8,128)}) custom-call(s32[4]{0:T(128)} %task_ref.3, bf16[128,2048]{1,0:T(8,128)(2,1)S(1)} %get-tuple-element.8.att_v, bf16[4,1024,128]{2,1,0:T(8,128)(2,1)S(1)} %get-tuple-element.9.gath_v), custom_call_target="tpu_custom_call" | custom-call | tf_op jit(solution)/shard_map/pallas_call | solution.py:494

commit v7 on v6

--- a/solution.py
+++ b/solution.py
@@ -361,6 +361,37 @@
 
     @pl.loop(1, n)
     def _(d):
+        dst = other(d, me, n)
+        seg_copy(me, dst).wait_send()
+        grs_copy(me, dst).wait_send()
+
+    swap_copy().wait_send()
+    pl.when(hi + 1 < n_hi)(lambda: w_copy().wait_send())
+    back_copy(lo).wait_send()
+
+    @pl.loop(1, n_hi)
+    def _(d):
+        dst = other(d, hi, n_hi)
+        prs_copy(hi, dst).wait_send()
+        pag_copy(hi, dst).wait_send()
+
+    for j in range(2):
+        @pl.when(jnp.logical_or(lo == 0, hi == 0) if j else lo == 0)
+        def _():
+            x_copy(own[j], hi, j, lo).wait_send()
+
+        @pl.loop(j, hi)
+        def _(blk):
+            x_copy(own[j], blk, j, lo).wait_send()
+
+        @pl.when(hi + 1 < n_hi)
+        def _():
+            @pl.loop(0, hi + 1)
+            def _(blk):
+                z_copy(own[j], blk, j).wait_send()
+
+    @pl.loop(1, n)
+    def _(d):
         src = other(d, me, n)
         gag_copy(src, me).wait_recv()
         pass_on(src)
@@ -385,35 +416,7 @@
 
     @pl.loop(1, n)
     def _(d):
-        dst = other(d, me, n)
-        seg_copy(me, dst).wait_send()
-        grs_copy(me, dst).wait_send()
-        gag_copy(me, dst).wait_send()
-
-    swap_copy().wait_send()
-    pl.when(hi + 1 < n_hi)(lambda: w_copy().wait_send())
-    back_copy(lo).wait_send()
-
-    @pl.loop(1, n_hi)
-    def _(d):
-        dst = other(d, hi, n_hi)
-        prs_copy(hi, dst).wait_send()
-        pag_copy(hi, dst).wait_send()
-
-    for j in range(2):
-        @pl.when(jnp.logical_or(lo == 0, hi == 0) if j else lo == 0)
-        def _():
-            x_copy(own[j], hi, j, lo).wait_send()
-
-        @pl.loop(j, hi)
-        def _(blk):
-            x_copy(own[j], blk, j, lo).wait_send()
-
-        @pl.when(hi + 1 < n_hi)
-        def _():
-            @pl.loop(0, hi + 1)
-            def _(blk):
-                z_copy(own[j], blk, j).wait_send()
+        gag_copy(me, other(d, me, n)).wait_send()
 
     @pl.loop(0, n)
     def _(j):

time: 60.3 us -> 60.1 us (level)
  no operation moved by 1% of the time
where the time goes in v7:
time: 60.1 us; the launch traced here: 60 us
  Pallas kernels  59.3 us (99%)
  between operations  0.64 us (1%)
    pallas_call x1, Pallas kernels, shards(): pl.pallas_call(functools.partial(kernel, n, n_dp), out_shape=(pltpu.VMEM(...  57.5 us
    pallas_call x1, Pallas kernels, shards(): pl.pallas_call(functools.partial(finish, n_dp), out_shape=(jax.ShapeDtype...  1.85 us

profile of v7, /device:TPU:1, one launch (start us, length us, event | category | flops | bytes accessed | tf_op | source)
XLA Modules:
  0.0 60.0 jit_solution(4186383132638072297)
XLA Ops:
  0.6 57.5 %shard_map.103 = (bf16[128,2048]{1,0:T(8,128)(2,1)S(1)}, bf16[4,1024,128]{2,1,0:T(8,128)(2,1)S(1)}) custom-call(s32[4]{0:T(128)} %task_ref.3, bf16[128,2048]{1,0:T(8,128)(2,1)} %bitcast.5, bf16[128,512]{1,0:T(8,128)(2,1)} %bitcast.7, bf16[128,512]{1,0:T(8,128)(2,1)} %bitcast.8, s32[1,128]{1,0:T(1,128)} %refs_3_.1, bf16[2,128,512]{2,1,0:T(8,128)(2,1)} %refs_4_.1, ...), custom_call_target="tpu_custom_call" | custom-call | tf_op jit(solution)/shard_map/pallas_call | solution.py:462
  58.1 1.9 %shard_map.104 = (bf16[128,2048]{1,0:T(8,128)(2,1)}, f32[2,128,512]{2,1,0:T(8,128)}, f32[2,128,512]{2,1,0:T(8,128)}) custom-call(s32[4]{0:T(128)} %task_ref.3, bf16[128,2048]{1,0:T(8,128)(2,1)S(1)} %get-tuple-element.8.att_v, bf16[4,1024,128]{2,1,0:T(8,128)(2,1)S(1)} %get-tuple-element.9.gath_v), custom_call_target="tpu_custom_call" | custom-call | tf_op jit(solution)/shard_map/pallas_call | solution.py:497
